TPU v7x, 128 devices: a whole 4x4x4 slice. The times are simulated.
128 devices in a mesh: row: 8 (over x, core), col: 16 (over y, z).
Axes of the slice: x: 4, y: 4, z: 4, core: 2. Of those that a mesh axis runs over, the one named last changes fastest.
Arguments:
- tokens: bfloat16 [65536, 1024], P(('row', 'col')), may hold values from -6 to 6
- expert_ids: int32 [65536, 1], P(('row', 'col')), may hold values from 0 to 127; in each aligned block of 512 rows (0 to 511, 512 to 1023, ...) at most 8 rows name the same one
- gate_prob: float32 [65536], P(('row', 'col')), may hold values from 0.25 to 1
- norm_gain: float32 [1024], replicated, may hold values from 0.1 to 1.9
- weight_in: bfloat16 [128, 1024, 4096], P(('row', 'col')), may hold values from -0.1875 to 0.1875
- weight_out: bfloat16 [128, 4096, 1024], P(('row', 'col')), may hold values from -0.09375 to 0.09375
Outputs:
- mixed: bfloat16 [65536, 1024], P(('row', 'col'))
- routed: int32 [128], P(('row', 'col'))
Inputs may be any that keep to these rules, and one draw needn't show every extreme that they name: `expert_ids`: among the 512 tokens of one device no expert is chosen more than 8 times; some expert is chosen exactly 8 times by some device's tokens.
All inputs are finite; a program needn't handle non-finite values.
Results may differ from a plain program's by a relative error of at most 0.001.
The roundings to bfloat16 on the way count: a program that leaves them out, or rounds other values in their place, can miss the bound.
Values may be sent and summed in bfloat16 or wider, within the bound.
A program may use at most 64 MiB of HBM per device.

v0:
```python
import jax
import jax.numpy as jnp
from jax import lax
from jax.sharding import Mesh
from jax.sharding import PartitionSpec as P

ROW = ("row_0", "row_1")
COL = ("col_0", "col_1")
ROW_COL = ("row_0", "row_1", "col_0", "col_1")


def split_up(array, dim, peers):
    before, after = (array.shape[:dim], array.shape[dim + 1 :])
    return jnp.moveaxis(array.reshape(*before, peers, -1, *after), dim, 0)


def sent_and_summed(array, axis, dim):
    parts = split_up(array, dim, lax.axis_size(axis))
    arrived = lax.all_to_all(parts, axis, split_axis=0, concat_axis=0, tiled=True)
    return arrived.sum(axis=0)


def sum_in_two_steps(array, axes, dim):
    far, near = axes
    own = sent_and_summed(split_up(array, dim, lax.axis_size(far)), near, dim + 1)
    return jnp.sum(lax.all_to_all(own, far, 0, 0, tiled=True), axis=0)


def joined_along(parts, dim):
    shape = list(parts.shape[1:])
    shape[dim] *= parts.shape[0]
    return jnp.moveaxis(parts, 0, dim).reshape(shape)


def one_exchange(array, axis, axes, splits, concats):
    sizes = [lax.axis_size(a) for a in axes]
    parts = split_up(array, splits[0], sizes[0])
    parts = jnp.moveaxis(split_up(parts, splits[1] + 1, sizes[1]), 0, 1)
    inside = parts.shape[2:]
    parts = parts.reshape(-1, *inside)
    parts = lax.all_to_all(parts, axis, split_axis=0, concat_axis=0, tiled=True)
    parts = joined_along(parts.reshape(*sizes, *inside), concats[0] + 1)
    return joined_along(parts, concats[1])


def slot_rank(block_ids):
    count = block_ids.shape[0]
    same = block_ids[:, None] == block_ids[None, :]
    earlier = (
        jnp.arange(count, dtype=jnp.int32)[None, :] < jnp.arange(count, dtype=jnp.int32)[:, None]
    )
    return jnp.sum((same & earlier).astype(jnp.int32), axis=1)


def run_expert(received, first, second):
    lead = received.shape[:-1]
    width = received.shape[-1]
    flat_rows = received.reshape(-1, width)
    hidden = jnp.maximum(jnp.dot(flat_rows, first, preferred_element_type=jnp.float32), 0.0).astype(
        jnp.bfloat16
    )
    answer = jnp.dot(hidden, second, preferred_element_type=jnp.float32).astype(jnp.bfloat16)
    return answer.reshape(lead + (width,))


def on_device(tokens, expert_ids, gate_prob, norm_gain, weight_in, weight_out):
    tok_rows, width = tokens.shape
    row_count = lax.axis_size(ROW)
    col_count = lax.axis_size(COL)
    experts = row_count * col_count
    capacity = 2 * tok_rows // experts
    local_ids = expert_ids[:, 0]
    within = slot_rank(local_ids)
    placed = local_ids * capacity + within
    wide = tokens.astype(jnp.float32)
    scale = lax.rsqrt(jnp.mean(wide * wide, axis=1, keepdims=True) + 1e-06)
    normed = (wide * scale * norm_gain[None, :]).astype(jnp.bfloat16)
    matches = (local_ids[:, None] == jnp.arange(experts, dtype=jnp.int32)[None, :]).astype(
        jnp.float32
    )
    counts = jnp.sum(matches, axis=0)
    routed = sum_in_two_steps(counts, (("row_0", "row_1", "col_0"), "col_1"), 0).astype(jnp.int32)
    table = (placed[None, :] == jnp.arange(experts * capacity, dtype=jnp.int32)[:, None]).astype(
        jnp.bfloat16
    )
    outgoing = jnp.dot(table, normed, preferred_element_type=jnp.float32).astype(jnp.bfloat16)
    first = weight_in[0]
    second = weight_out[0]
    grid_out = outgoing.reshape(row_count, col_count, capacity, width)
    arrived = one_exchange(grid_out, ROW_COL, (ROW, COL), (0, 1), (0, 1))
    answers = run_expert(arrived, first, second)
    returned = one_exchange(answers, ROW_COL, (ROW, COL), (0, 1), (0, 1))
    returned = returned.reshape(experts * capacity, width)
    back = jnp.einsum("st,sd->td", table, returned, preferred_element_type=jnp.float32)
    mixed = (wide + gate_prob[:, None] * back).astype(jnp.bfloat16)
    return (mixed, routed)


def solution(mesh):
    finer = Mesh(mesh.devices.reshape(4, 2, 4, 4), ("row_0", "row_1", "col_0", "col_1"))
    return jax.shard_map(
        on_device,
        mesh=finer,
        in_specs=(
            P(ROW_COL, None),
            P(ROW_COL, None),
            P(ROW_COL),
            P(),
            P(ROW_COL, None, None),
            P(ROW_COL, None, None),
        ),
        out_specs=(P(ROW_COL, None), P(ROW_COL)),
        check_vma=False,
    )
```

profile of v0, /device:TPU:1, one launch (start us, length us, event | category | flops | bytes accessed | tf_op | source)
XLA Modules:
  0.0 124.9 jit_solution(17238979280621386907)
XLA Ops:
  0.6 0.8 convert_reduce_fusion.1
  1.5 0.1 reshape_reshape.11
  1.6 0.7 copy.14
  2.2 5.8 %all-to-all-start.2 = ((f32[4,32,1]{1,2,0:T(1,128)}), f32[4,32,1]{1,2,0:T(1,128)S(1)}, u32[]{:S(2)}, u32[]{:S(2)}) async-start(f32[4,32,1]{1,2,0:T(1,128)} %copy.14), calls=%async_computation.2 | async-start | bytes 4096 | tf_op jit(solution)/shard_map/all_to_all | solution.py:19
  8.1 1.0 convert_reduce_fusion
  9.1 0.7 multiply_add_fusion
  9.8 1.5 %fusion.5 = f32[512]{0:T(512)S(1)} fusion(bf16[512,1024]{1,0:T(8,128)(2,1)} %param.6), kind=kLoop, calls=%fused_computation.7 | loop fusion | flops 1572352 | bytes 1050624 | tf_op jit(solution)/shard_map/reduce_sum | solution.py:76
  11.3 4.0 %convert_bitcast_fusion.1 = bf16[128,1,1,8,1024]{4,3,2,1,0:T(8,128)(2,1)} fusion(bf16[512,1024]{1,0:T(8,128)(2,1)} %param.6, f32[1024]{0:T(1024)} %param.9, f32[512]{0:T(512)S(1)} %add_rsqrt_fusion, s32[512]{0:T(512)S(1)} %multiply_add_fusion), kind=kOutput, calls=%fused_computation.15 | convolution fusion | flops 1077411840 | bytes 3153920 | tf_op jit(solution)/shard_map/dot_general | solution.py:86
  15.3 0.0 all-to-all-done.2
  15.3 10.4 %all-to-all-start = ((bf16[128,1,1,8,1024]{4,3,2,1,0:T(8,128)(2,1)}), bf16[128,1,1,8,1024]{4,3,2,1,0:T(8,128)(2,1)S(1)}, u32[]{:S(2)}, u32[]{:S(2)}) async-start(bf16[128,1,1,8,1024]{4,3,2,1,0:T(8,128)(2,1)} %convert_bitcast_fusion.1), calls=%async_computation | async-start | bytes 4194304 | tf_op jit(solution)/shard_map/all_to_all | solution.py:41
  25.7 0.7 copy.15
  26.4 28.6 %all-to-all-done = bf16[128,1,1,8,1024]{4,3,2,1,0:T(8,128)(2,1)S(1)} async-done(((bf16[128,1,1,8,1024]{4,3,2,1,0:T(8,128)(2,1)}), bf16[128,1,1,8,1024]{4,3,2,1,0:T(8,128)(2,1)S(1)}, u32[]{:S(2)}, u32[]{:S(2)}) %all-to-all-start) | async-done | bytes 2097184 | tf_op jit(solution)/shard_map/all_to_all | solution.py:41
  55.1 5.2 %all-to-all-start.3 = ((f32[32,1,1]{2,1,0:T(1,128)}), f32[32,1,1]{2,1,0:T(1,128)S(1)}, u32[]{:S(2)}, u32[]{:S(2)}) async-start(f32[32,1,1]{2,1,0:T(1,128)} %copy.15), calls=%async_computation.3 | async-start | bytes 32768 | tf_op jit(solution)/shard_map/all_to_all | solution.py:26
  60.3 24.6 %convert_bitcast_fusion = bf16[128,1,1,8,1024]{4,3,2,1,0:T(8,128)(2,1)} fusion(bf16[1,4096,1024]{2,1,0:T(8,128)(2,1)} %param.11, bf16[1,1024,4096]{2,1,0:T(8,128)(2,1)} %param.10, bf16[128,1,1,8,1024]{4,3,2,1,0:T(8,128)(2,1)S(1)} %all-to-all-done), kind=kOutput, calls=%fused_computation.14 | convolution fusion | flops 17189306368 | bytes 20971520 | tf_op jit(solution)/shard_map/dot_general | solution.py:62
  84.8 0.0 copy-start
  84.8 0.0 copy-start.1
  84.9 0.0 all-to-all-done.3
  84.9 7.3 %all-to-all-start.1 = ((bf16[128,1,1,8,1024]{4,3,2,1,0:T(8,128)(2,1)}), bf16[128,1,1,8,1024]{4,3,2,1,0:T(8,128)(2,1)S(1)}, u32[]{:S(2)}, u32[]{:S(2)}) async-start(bf16[128,1,1,8,1024]{4,3,2,1,0:T(8,128)(2,1)} %convert_bitcast_fusion), calls=%async_computation.1 | async-start | bytes 4194304 | tf_op jit(solution)/shard_map/all_to_all | solution.py:41
  92.2 0.6 reduce_sum.49
  93.5 28.1 %all-to-all-done.1 = bf16[128,1,1,8,1024]{4,3,2,1,0:T(8,128)(2,1)S(1)} async-done(((bf16[128,1,1,8,1024]{4,3,2,1,0:T(8,128)(2,1)}), bf16[128,1,1,8,1024]{4,3,2,1,0:T(8,128)(2,1)S(1)}, u32[]{:S(2)}, u32[]{:S(2)}) %all-to-all-start.1) | async-done | bytes 2097184 | tf_op jit(solution)/shard_map/all_to_all | solution.py:41
  121.5 0.0 copy-done
  121.5 0.0 copy-done.1
  121.5 2.3 %fusion.8 = bf16[512,1024]{1,0:T(8,128)(2,1)} fusion(bf16[512,1024]{1,0:T(8,128)(2,1)S(1)} %copy-done, bf16[128,1,1,8,1024]{4,3,2,1,0:T(8,128)(2,1)S(1)} %all-to-all-done.1, s32[512]{0:T(512)S(1)} %multiply_add_fusion, f32[512]{0:T(512)S(1)} %copy-done.1), kind=kOutput, calls=%fused_computation.10 | convolution fusion | flops 1076363264 | bytes 4198400 | tf_op jit(solution)/shard_map/st,sd->td/dot_general | solution.py:94
  (2 shorter events, 0.0 us)
Async XLA Ops:
  2.2 13.0 %all-to-all-start.2 = ((f32[4,32,1]{1,2,0:T(1,128)}), f32[4,32,1]{1,2,0:T(1,128)S(1)}, u32[]{:S(2)}, u32[]{:S(2)}) async-start(f32[4,32,1]{1,2,0:T(1,128)} %copy.14), calls=%async_computation.2 | async-start | bytes 4096 | tf_op jit(solution)/shard_map/all_to_all | solution.py:19
  15.3 39.8 %all-to-all-start = ((bf16[128,1,1,8,1024]{4,3,2,1,0:T(8,128)(2,1)}), bf16[128,1,1,8,1024]{4,3,2,1,0:T(8,128)(2,1)S(1)}, u32[]{:S(2)}, u32[]{:S(2)}) async-start(bf16[128,1,1,8,1024]{4,3,2,1,0:T(8,128)(2,1)} %convert_bitcast_fusion.1), calls=%async_computation | async-start | bytes 4194304 | tf_op jit(solution)/shard_map/all_to_all | solution.py:41
  55.1 29.8 %all-to-all-start.3 = ((f32[32,1,1]{2,1,0:T(1,128)}), f32[32,1,1]{2,1,0:T(1,128)S(1)}, u32[]{:S(2)}, u32[]{:S(2)}) async-start(f32[32,1,1]{2,1,0:T(1,128)} %copy.15), calls=%async_computation.3 | async-start | bytes 32768 | tf_op jit(solution)/shard_map/all_to_all | solution.py:26
  84.8 36.7 %copy-start = (bf16[512,1024]{1,0:T(8,128)(2,1)S(1)}, bf16[512,1024]{1,0:T(8,128)(2,1)}, u32[]{:S(2)}) copy-start(bf16[512,1024]{1,0:T(8,128)(2,1)} %param.6) | copy-start | bytes 3145732
  84.8 36.7 %copy-start.1 = (f32[512]{0:T(512)S(1)}, f32[512]{0:T(512)}, u32[]{:S(2)}) copy-start(f32[512]{0:T(512)} %param.8) | copy-start | bytes 6148
  84.9 36.7 %all-to-all-start.1 = ((bf16[128,1,1,8,1024]{4,3,2,1,0:T(8,128)(2,1)}), bf16[128,1,1,8,1024]{4,3,2,1,0:T(8,128)(2,1)S(1)}, u32[]{:S(2)}, u32[]{:S(2)}) async-start(bf16[128,1,1,8,1024]{4,3,2,1,0:T(8,128)(2,1)} %convert_bitcast_fusion), calls=%async_computation.1 | async-start | bytes 4194304 | tf_op jit(solution)/shard_map/all_to_all | solution.py:41
where the time goes:
time: 126 us; the launch traced here: 125 us
  waiting for transfers between devices  56.7 us (45%)
  matrix products  30.8 us (24%)
  starting transfers between devices  28.8 us (23%)
  other arithmetic  4.69 us (4%)
  between operations  2.46 us (2%)
  local copies, waits for them, and re-layouts  1.46 us (1%)
    all_to_all x2, waiting for transfers between devices, one_exchange(): parts = lax.all_to_all(parts, axis, split_axis=0, concat_axis=0, tiled=True)  56.7 us
    dot_general x1, matrix products, run_expert(): jnp.dot(hidden, second, preferred_element_type=jnp.float32)  24.6 us
    all_to_all x2, starting transfers between devices, one_exchange(): parts = lax.all_to_all(parts, axis, split_axis=0, concat_axis=0, tiled=True)  17.7 us
    all_to_all x1, starting transfers between devices, sent_and_summed(): lax.all_to_all(parts, axis, split_axis=0, concat_axis=0, tiled=True)  5.84 us
    all_to_all x1, starting transfers between devices, sum_in_two_steps(): return jnp.sum(lax.all_to_all(own, far, 0, 0, tiled=True), axis=0)  5.19 us
    dot_general x1, matrix products, on_device(): jnp.dot(table, normed, preferred_element_type=jnp.float32)  3.98 us
  transfers between devices with their start and end apart: 4, of which 2 were waited for; matrix products, arithmetic and copies ran while one was open for 27% of the time, Pallas kernels for 0%

commit v1 on v0

v1 whole, which is shorter than its diff:
```python
import functools

import jax
import jax.numpy as jnp
from jax import lax
from jax.experimental import pallas as pl
from jax.experimental.pallas import tpu as pltpu
from jax.sharding import PartitionSpec as P

ROW_COL = ("row", "col")
MESH = pl.DeviceIdType.MESH
TOK = 512
D = 1024
FF = 4096
CAP = 8
PEERS = 128
CHUNKS = 4
GROUP = PEERS // CHUNKS
ROWS = GROUP * CAP
SLOTS = PEERS * CAP
EMPTY = 1024.0
FF_TILE = 512
D_TILE = 256


def place():
    r = lax.axis_index("row")
    c = lax.axis_index("col")
    return lax.div(r, 2), lax.rem(r, 2), lax.div(c, 4), lax.rem(c, 4)


def peer(spot, chunk, i, sign):
    x, core, y, z = spot
    dx, dy, dc = lax.div(i, 8), lax.rem(lax.div(i, 2), 4), lax.rem(i, 2)
    dz = lax.rem(chunk + 8 - dx - dy, 4)
    if sign < 0:
        dx, dy, dz = 4 - dx, 4 - dy, 4 - dz
    row = lax.rem(x + dx, 4) * 2 + lax.rem(core + dc, 2)
    col = lax.rem(y + dy, 4) * 4 + lax.rem(z + dz, 4)
    return row, col


def kernel(
    tok_ref,
    ids_ref,
    gate_ref,
    gain_ref,
    w1_hbm,
    w2_hbm,
    out_ref,
    routed_ref,
    w1,
    w2,
    normed,
    slot_cols,
    outgoing,
    arrived,
    answers,
    returned,
    hidden,
    total,
    w_sem,
    send_out,
    recv_out,
    send_back,
    recv_back,
):
    spot = place()
    x, core, y, z = spot
    load1 = pltpu.make_async_copy(w1_hbm.at[0], w1, w_sem.at[0])
    load2 = pltpu.make_async_copy(w2_hbm.at[0], w2, w_sem.at[1])
    load1.start()
    load2.start()
    barrier = pltpu.get_barrier_semaphore()
    for chunk in range(CHUNKS):

        def greet(i, carry, chunk=chunk):
            pl.semaphore_signal(barrier, inc=1, device_id=peer(spot, chunk, i, 1), device_id_type=MESH)
            return carry

        lax.fori_loop(1 if chunk == 0 else 0, GROUP, greet, 0)

    ids_row = ids_ref[...]
    ids_cols = jnp.broadcast_to(ids_row, (128, TOK)).T
    parts = []
    for j in range(TOK // 128):
        mine = ids_row[:, j * 128 : (j + 1) * 128]
        t = lax.broadcasted_iota(jnp.int32, (TOK, 128), 1) + j * 128
        before = lax.broadcasted_iota(jnp.int32, (TOK, 128), 0) < t
        hit = jnp.where((ids_cols == mine) & before, 1.0, 0.0)
        parts.append(jnp.sum(hit, axis=0, keepdims=True))
    within = jnp.concatenate(parts, axis=1).astype(jnp.int32)
    dx = ((ids_row >> 5) - x) & 3
    dc = ((ids_row >> 4) - core) & 1
    dy = ((ids_row >> 2) - y) & 3
    dz = (ids_row - z) & 3
    order = ((dx + dy + dz) & 3) * GROUP + dx * 8 + dy * 2 + dc
    slot_row = order * CAP + within
    slot_cols[...] = jnp.broadcast_to(slot_row, (128, TOK)).T

    for b in range(TOK // 128):
        rows = pl.ds(b * 128, 128)
        wide = tok_ref[rows, :].astype(jnp.float32)
        scale = lax.rsqrt(jnp.mean(wide * wide, axis=1, keepdims=True) + 1e-06)
        normed[rows, :] = (wide * scale * gain_ref[...]).astype(jnp.bfloat16)

    ones = jnp.ones((TOK, 128), jnp.bfloat16)
    for chunk in range(CHUNKS):
        base = chunk * ROWS
        place_at = lax.broadcasted_iota(jnp.int32, (ROWS, TOK), 0) + base
        table = jnp.where(slot_row == place_at, 1.0, 0.0).astype(jnp.bfloat16)
        filled = jnp.dot(table, ones, preferred_element_type=jnp.float32)
        values = jnp.dot(table, normed[...], preferred_element_type=jnp.float32)
        first_lane = lax.broadcasted_iota(jnp.int32, (ROWS, 128), 1) == 0
        head = jnp.where(first_lane & (filled == 0.0), EMPTY, values[:, :128])
        group = pl.ds(chunk * GROUP, GROUP)
        outgoing[group, :, :128] = head.astype(jnp.bfloat16).reshape(GROUP, CAP, 128)
        outgoing[group, :, 128:] = values[:, 128:].astype(jnp.bfloat16).reshape(GROUP, CAP, D - 128)
        if chunk == 0:
            pl.semaphore_wait(barrier, PEERS - 1)

        def send(i, carry, chunk=chunk):
            k = chunk * GROUP + i
            pltpu.make_async_remote_copy(
                src_ref=outgoing.at[k],
                dst_ref=arrived.at[k],
                send_sem=send_out.at[chunk],
                recv_sem=recv_out.at[chunk],
                device_id=peer(spot, chunk, i, 1),
                device_id_type=MESH,
            ).start()
            return carry

        lax.fori_loop(1 if chunk == 0 else 0, GROUP, send, 0)
    arrived[0] = outgoing[0]

    load1.wait()
    load2.wait()
    seen = jnp.zeros((1, 128), jnp.float32)
    for chunk in range(CHUNKS):
        skip = 1 if chunk == 0 else 0
        moved = pl.ds(chunk * GROUP + skip, GROUP - skip)
        pltpu.make_async_copy(outgoing.at[moved], arrived.at[moved], recv_out.at[chunk]).wait()
        group = pl.ds(chunk * GROUP, GROUP)
        head = arrived[group, :, :128].astype(jnp.float32).reshape(ROWS, 128)
        first_lane = lax.broadcasted_iota(jnp.int32, (ROWS, 128), 1) == 0
        full = jnp.where(first_lane & (head != EMPTY), 1.0, 0.0)
        seen += jnp.sum(full, axis=0, keepdims=True)
        block = arrived[group].reshape(ROWS, D)

        def up(j, carry, block=block):
            cols = pl.ds(pl.multiple_of(j * FF_TILE, FF_TILE), FF_TILE)
            h = jnp.dot(block, w1[:, cols], preferred_element_type=jnp.float32)
            hidden[:, cols] = jnp.maximum(h, 0.0).astype(jnp.bfloat16)
            return carry

        lax.fori_loop(0, FF // FF_TILE, up, 0)

        def down(j, carry, chunk=chunk):
            cols = pl.ds(pl.multiple_of(j * D_TILE, D_TILE), D_TILE)
            a = jnp.dot(hidden[...], w2[:, cols], preferred_element_type=jnp.float32)
            answers[pl.ds(chunk * GROUP, GROUP), :, cols] = a.astype(jnp.bfloat16).reshape(GROUP, CAP, D_TILE)
            return carry

        lax.fori_loop(0, D // D_TILE, down, 0)

        def reply(i, carry, chunk=chunk):
            k = chunk * GROUP + i
            pltpu.make_async_remote_copy(
                src_ref=answers.at[k],
                dst_ref=returned.at[k],
                send_sem=send_back.at[chunk],
                recv_sem=recv_back.at[chunk],
                device_id=peer(spot, chunk, i, -1),
                device_id_type=MESH,
            ).start()
            return carry

        lax.fori_loop(skip, GROUP, reply, 0)
        if chunk == 0:
            returned[0] = answers[0]
    routed_ref[0] = jnp.sum(seen).astype(jnp.int32)

    gate_cols = jnp.broadcast_to(gate_ref[...], (128, TOK)).T
    for chunk in range(CHUNKS):
        skip = 1 if chunk == 0 else 0
        moved = pl.ds(chunk * GROUP + skip, GROUP - skip)
        picks = []
        for j in range(ROWS // 128):
            lane = lax.broadcasted_iota(jnp.int32, (TOK, 128), 1) + (chunk * ROWS + j * 128)
            picks.append(jnp.where(slot_cols[...] == lane, 1.0, 0.0).astype(jnp.bfloat16))
        pick = jnp.concatenate(picks, axis=1)
        pltpu.make_async_copy(answers.at[moved], returned.at[moved], recv_back.at[chunk]).wait()
        block = returned[pl.ds(chunk * GROUP, GROUP)].reshape(ROWS, D)
        back = jnp.dot(pick, block, preferred_element_type=jnp.float32)
        if chunk == 0:
            total[...] = back
        elif chunk < CHUNKS - 1:
            total[...] += back
        else:
            for j in range(D // 128):
                cols = slice(j * 128, (j + 1) * 128)
                got = total[:, cols] + back[:, cols]
                out_ref[:, cols] = (tok_ref[:, cols].astype(jnp.float32) + gate_cols * got).astype(jnp.bfloat16)
    for chunk in range(CHUNKS):
        skip = 1 if chunk == 0 else 0
        moved = pl.ds(chunk * GROUP + skip, GROUP - skip)
        pltpu.make_async_copy(outgoing.at[moved], arrived.at[moved], send_out.at[chunk]).wait()
        pltpu.make_async_copy(answers.at[moved], returned.at[moved], send_back.at[chunk]).wait()


def on_device(tokens, expert_ids, gate_prob, norm_gain, weight_in, weight_out):
    vmem = pl.BlockSpec(memory_space=pltpu.VMEM)
    hbm = pl.BlockSpec(memory_space=pl.ANY)
    slab = pltpu.VMEM((PEERS, CAP, D), jnp.bfloat16)
    mixed, routed = pl.pallas_call(
        kernel,
        out_shape=(
            jax.ShapeDtypeStruct((TOK, D), jnp.bfloat16),
            jax.ShapeDtypeStruct((1,), jnp.int32),
        ),
        in_specs=[vmem, vmem, vmem, vmem, hbm, hbm],
        out_specs=(vmem, pl.BlockSpec(memory_space=pltpu.SMEM)),
        scratch_shapes=[
            pltpu.VMEM((D, FF), jnp.bfloat16),
            pltpu.VMEM((FF, D), jnp.bfloat16),
            pltpu.VMEM((TOK, D), jnp.bfloat16),
            pltpu.VMEM((TOK, 128), jnp.int32),
            slab,
            slab,
            slab,
            slab,
            pltpu.VMEM((ROWS, FF), jnp.bfloat16),
            pltpu.VMEM((TOK, D), jnp.float32),
            pltpu.SemaphoreType.DMA((2,)),
            pltpu.SemaphoreType.DMA((CHUNKS,)),
            pltpu.SemaphoreType.DMA((CHUNKS,)),
            pltpu.SemaphoreType.DMA((CHUNKS,)),
            pltpu.SemaphoreType.DMA((CHUNKS,)),
        ],
        compiler_params=pltpu.CompilerParams(
            collective_id=0, has_side_effects=True, vmem_limit_bytes=56 * 2**20
        ),
    )(
        tokens,
        expert_ids.reshape(1, TOK),
        gate_prob.reshape(1, TOK),
        norm_gain.reshape(1, D),
        weight_in,
        weight_out,
    )
    return mixed, routed


def solution(mesh):
    return jax.shard_map(
        on_device,
        mesh=mesh,
        in_specs=(
            P(ROW_COL, None),
            P(ROW_COL, None),
            P(ROW_COL),
            P(),
            P(ROW_COL, None, None),
            P(ROW_COL, None, None),
        ),
        out_specs=(P(ROW_COL, None), P(ROW_COL)),
        check_vma=False,
    )
```

time: 126 us -> 70.6 us (0.56)
  Pallas kernels: 0 us -> 65.8 us
  waiting for transfers between devices: 56.7 us -> 0 us
  matrix products: 30.8 us -> 0 us
  starting transfers between devices: 28.8 us -> 0 us
  other arithmetic: 4.69 us -> 0 us
    pallas_call x0 -> x1, Pallas kernels: none -> 65.8 us  [on_device(): pl.pallas_call(kernel, out_shape=(jax.ShapeDtypeStruct((TOK, D), jnp.bflo...]
    all_to_all x4 -> x0, waiting for transfers between devices: 56.7 us -> none  [the longest x2 56.7 us: one_exchange(): parts = lax.all_to_all(parts, axis, split_axis=0, concat_axis=0, tiled=True)]
    dot_general x3 -> x0, matrix products: 30.8 us -> none  [the longest x1 24.6 us: run_expert(): jnp.dot(hidden, second, preferred_element_type=jnp.float32)]
    all_to_all x4 -> x0, starting transfers between devices: 28.8 us -> none  [the longest x2 17.7 us: one_exchange(): parts = lax.all_to_all(parts, axis, split_axis=0, concat_axis=0, tiled=True)]
    reduce_sum x5 -> x0, other arithmetic: 3.99 us -> none  [the longest x1 1.5 us: on_device(): scale = lax.rsqrt(jnp.mean(wide * wide, axis=1, keepdims=True) + 1e-06)]
    unnamed x4 -> x1, local copies, waits for them, and re-layouts: 0.01 us -> 2.26 us
  transfers between devices with their start and end apart: 4 -> 0, of which waited for: 2 -> 0; matrix products, arithmetic and copies ran while one was open for 27% -> 0% of each run, Pallas kernels for 0% -> 0%
where the time goes in v1:
time: 70.6 us; the launch traced here: 70.4 us
  Pallas kernels  65.8 us (93%)
  between operations  2.33 us (3%)
  local copies, waits for them, and re-layouts  2.26 us (3%)
    pallas_call x1, Pallas kernels, on_device(): pl.pallas_call(kernel, out_shape=(jax.ShapeDtypeStruct((TOK, D), jnp.bflo...  65.8 us
    unnamed x1, local copies, waits for them, and re-layouts  2.26 us

profile of v1, /device:TPU:1, one launch (start us, length us, event | category | flops | bytes accessed | tf_op | source)
XLA Modules:
  0.0 70.4 jit_solution(12021589180403408737)
XLA Ops:
  0.6 65.8 %shard_map.77 = (bf16[512,1024]{1,0:T(8,128)(2,1)}, s32[1]{0:T(128)}) custom-call(bf16[512,1024]{1,0:T(8,128)(2,1)} %tok_ref.1, s32[1,512]{1,0:T(1,128)} %bitcast.4, f32[1,512]{1,0:T(1,128)} %bitcast.5, f32[1,1024]{1,0:T(1,128)} %bitcast.3, bf16[1,1024,4096]{2,1,0:T(8,128)(2,1)} %w1_hbm.1, bf16[1,4096,1024]{2,1,0:T(8,128)(2,1)} %w2_hbm.1), custom_call_target="tpu_custom_call" | custom-call | tf_op jit(solution)/shard_map/pallas_call | solution.py:216
  66.4 2.3 %copy.10 = bf16[512,1024]{1,0:T(8,128)(2,1)} copy(bf16[512,1024]{1,0:T(8,128)(2,1)} %get-tuple-element.4) | data formatting | bytes 2097152

commit v2 on v1

v2 whole, which is shorter than its diff:
```python
import jax
import jax.numpy as jnp
from jax import lax
from jax.experimental import pallas as pl
from jax.experimental.pallas import tpu as pltpu
from jax.sharding import PartitionSpec as P

ROW_COL = ("row", "col")
MESH = pl.DeviceIdType.MESH
TOK = 512
D = 1024
FF = 4096
CAP = 8
PEERS = 128
SLOTS = PEERS * CAP
CLASSES = 4
CLASS = PEERS // CLASSES
GROUPS = ((0, 32), (32, 32), (64, 32), (96, 32))
MOST = max(count for _, count in GROUPS) * CAP
EMPTY = 1024.0
FF_TILE = 512
D_TILE = 256
LANES = 128
VMEM_LIMIT = 44 * 2**20


def offset(k):
    dx, dy, dc = k // 8 % 4, k // 2 % 4, k % 2
    return dx, dy, (k // CLASS - dx - dy) % 4, dc


def hops(k):
    return sum(min(d, 4 - d) for d in offset(k)[:3])


FAR_FIRST = sorted(range(1, PEERS), key=lambda k: -hops(k))


class Place:
    def __init__(self):
        r = lax.axis_index("row")
        c = lax.axis_index("col")
        self.x, self.core = lax.div(r, 2), lax.rem(r, 2)
        self.y, self.z = lax.div(c, 4), lax.rem(c, 4)
        self.xs = [lax.rem(self.x + d, 4) * 2 for d in range(4)]
        self.cores = [lax.rem(self.core + d, 2) for d in range(2)]
        self.ys = [lax.rem(self.y + d, 4) * 4 for d in range(4)]
        self.zs = [lax.rem(self.z + d, 4) for d in range(4)]

    def peer(self, k, sign):
        dx, dy, dz, dc = offset(k)
        if sign < 0:
            dx, dy, dz = -dx % 4, -dy % 4, -dz % 4
        return self.xs[dx] + self.cores[dc], self.ys[dy] + self.zs[dz]


def group_of(k):
    return next(g for g, (first, count) in enumerate(GROUPS) if first <= k < first + count)


def moved(g):
    first, count = GROUPS[g]
    skip = 1 if first == 0 else 0
    return pl.ds(first + skip, count - skip)


def columns(row):
    return jnp.broadcast_to(row, (LANES, TOK)).T


def kernel(
    tok_hbm,
    ids_hbm,
    gate_hbm,
    gain_hbm,
    w1_hbm,
    w2_hbm,
    out_ref,
    routed_ref,
    tok,
    ids,
    gate,
    gain,
    w1,
    w2,
    normed,
    slot_cols,
    outgoing,
    arrived,
    answers,
    returned,
    hidden,
    total,
    load_sem,
    send_out,
    recv_out,
    send_back,
    recv_back,
):
    here = Place()
    loads = [
        pltpu.make_async_copy(source, target, load_sem.at[n])
        for n, (source, target) in enumerate(
            [
                (ids_hbm, ids),
                (tok_hbm, tok),
                (gain_hbm, gain),
                (w1_hbm.at[0], w1),
                (w2_hbm.at[0], w2),
                (gate_hbm, gate),
            ]
        )
    ]
    for load in loads[:3]:
        load.start()
    barrier = pltpu.get_barrier_semaphore()
    for k in FAR_FIRST:
        pl.semaphore_signal(barrier, inc=1, device_id=here.peer(k, 1), device_id_type=MESH)
    for load in loads[3:]:
        load.start()

    loads[0].wait()
    ids_row = ids[...]
    ids_cols = columns(ids_row)
    parts = []
    for j in range(TOK // LANES):
        mine = ids_row[:, j * LANES : (j + 1) * LANES]
        t = lax.broadcasted_iota(jnp.int32, (TOK, LANES), 1) + j * LANES
        before = lax.broadcasted_iota(jnp.int32, (TOK, LANES), 0) < t
        hit = jnp.where((ids_cols == mine) & before, 1.0, 0.0)
        parts.append(jnp.sum(hit, axis=0, keepdims=True))
    within = jnp.concatenate(parts, axis=1).astype(jnp.int32)
    dx = ((ids_row >> 5) - here.x) & 3
    dc = ((ids_row >> 4) - here.core) & 1
    dy = ((ids_row >> 2) - here.y) & 3
    dz = (ids_row - here.z) & 3
    slot_row = (((dx + dy + dz) & 3) * CLASS + dx * 8 + dy * 2 + dc) * CAP + within
    slot_cols[...] = columns(slot_row)

    loads[1].wait()
    loads[2].wait()
    for b in range(TOK // LANES):
        rows = pl.ds(b * LANES, LANES)
        wide = tok[rows, :].astype(jnp.float32)
        scale = lax.rsqrt(jnp.mean(wide * wide, axis=1, keepdims=True) + 1e-06)
        normed[rows, :] = (wide * scale * gain[...]).astype(jnp.bfloat16)

    ones = jnp.ones((TOK, LANES), jnp.bfloat16)
    rows = CLASS * CAP
    for c in range(CLASSES):
        places = lax.broadcasted_iota(jnp.int32, (rows, TOK), 0) + c * rows
        table = jnp.where(slot_row == places, 1.0, 0.0).astype(jnp.bfloat16)
        filled = jnp.dot(table, ones, preferred_element_type=jnp.float32)
        values = jnp.dot(table, normed[...], preferred_element_type=jnp.float32)
        first_lane = lax.broadcasted_iota(jnp.int32, (rows, LANES), 1) == 0
        head = jnp.where(first_lane & (filled == 0.0), EMPTY, values[:, :LANES])
        part = pl.ds(c * CLASS, CLASS)
        outgoing[part, :, :LANES] = head.astype(jnp.bfloat16).reshape(CLASS, CAP, LANES)
        outgoing[part, :, LANES:] = values[:, LANES:].astype(jnp.bfloat16).reshape(CLASS, CAP, D - LANES)
        if c == 0:
            pl.semaphore_wait(barrier, PEERS - 1)
        for k in range(max(c * CLASS, 1), (c + 1) * CLASS):
            pltpu.make_async_remote_copy(
                src_ref=outgoing.at[k],
                dst_ref=arrived.at[k],
                send_sem=send_out.at[group_of(k)],
                recv_sem=recv_out.at[group_of(k)],
                device_id=here.peer(k, 1),
                device_id_type=MESH,
            ).start()
    arrived[0] = outgoing[0]

    seen = jnp.zeros((1, LANES), jnp.float32)
    for g, (first, count) in enumerate(GROUPS):
        rows = count * CAP
        if g == 0:
            loads[3].wait()
            loads[4].wait()
        pltpu.make_async_copy(outgoing.at[moved(g)], arrived.at[moved(g)], recv_out.at[g]).wait()
        part = pl.ds(first, count)
        head = arrived[part, :, :LANES].astype(jnp.float32).reshape(rows, LANES)
        first_lane = lax.broadcasted_iota(jnp.int32, (rows, LANES), 1) == 0
        seen += jnp.sum(jnp.where(first_lane & (head != EMPTY), 1.0, 0.0), axis=0, keepdims=True)
        block = arrived[part].reshape(rows, D)

        def up(j, carry, block=block, rows=rows):
            cols = pl.ds(pl.multiple_of(j * FF_TILE, FF_TILE), FF_TILE)
            h = jnp.dot(block, w1[:, cols], preferred_element_type=jnp.float32)
            hidden[:rows, cols] = jnp.maximum(h, 0.0).astype(jnp.bfloat16)
            return carry

        lax.fori_loop(0, FF // FF_TILE, up, 0)

        def down(j, carry, part=part, count=count, rows=rows):
            cols = pl.ds(pl.multiple_of(j * D_TILE, D_TILE), D_TILE)
            a = jnp.dot(hidden[:rows], w2[:, cols], preferred_element_type=jnp.float32)
            answers[part, :, cols] = a.astype(jnp.bfloat16).reshape(count, CAP, D_TILE)
            return carry

        lax.fori_loop(0, D // D_TILE, down, 0)
        for k in range(max(first, 1), first + count):
            pltpu.make_async_remote_copy(
                src_ref=answers.at[k],
                dst_ref=returned.at[k],
                send_sem=send_back.at[g],
                recv_sem=recv_back.at[g],
                device_id=here.peer(k, -1),
                device_id_type=MESH,
            ).start()
        if g == 0:
            returned[0] = answers[0]
    routed_ref[0] = jnp.sum(seen).astype(jnp.int32)

    loads[5].wait()
    gate_cols = columns(gate[...])
    for g, (first, count) in enumerate(GROUPS):
        picks = []
        for j in range(count * CAP // LANES):
            lane = lax.broadcasted_iota(jnp.int32, (TOK, LANES), 1) + (first * CAP + j * LANES)
            picks.append(jnp.where(slot_cols[...] == lane, 1.0, 0.0).astype(jnp.bfloat16))
        pick = jnp.concatenate(picks, axis=1)
        pltpu.make_async_copy(answers.at[moved(g)], returned.at[moved(g)], recv_back.at[g]).wait()
        block = returned[pl.ds(first, count)].reshape(count * CAP, D)
        back = jnp.dot(pick, block, preferred_element_type=jnp.float32)
        if g == 0:
            total[...] = back
        elif g < len(GROUPS) - 1:
            total[...] += back
        else:
            for j in range(D // LANES):
                cols = slice(j * LANES, (j + 1) * LANES)
                got = gate_cols * (total[:, cols] + back[:, cols])
                out_ref[:, cols] = (tok[:, cols].astype(jnp.float32) + got).astype(jnp.bfloat16)
    for g in range(len(GROUPS)):
        pltpu.make_async_copy(outgoing.at[moved(g)], arrived.at[moved(g)], send_out.at[g]).wait()
        pltpu.make_async_copy(answers.at[moved(g)], returned.at[moved(g)], send_back.at[g]).wait()


def put_out(mixed, count, mixed_out, count_out, sem):
    first = pltpu.make_async_copy(mixed, mixed_out, sem.at[0])
    second = pltpu.make_async_copy(count, count_out, sem.at[1])
    first.start()
    second.start()
    first.wait()
    second.wait()


def on_device(tokens, expert_ids, gate_prob, norm_gain, weight_in, weight_out):
    vmem = pl.BlockSpec(memory_space=pltpu.VMEM)
    smem = pl.BlockSpec(memory_space=pltpu.SMEM)
    hbm = pl.BlockSpec(memory_space=pltpu.HBM)
    outs = (jax.ShapeDtypeStruct((TOK, D), jnp.bfloat16), jax.ShapeDtypeStruct((1,), jnp.int32))
    slab = pltpu.VMEM((PEERS, CAP, D), jnp.bfloat16)
    sems = pltpu.SemaphoreType.DMA((len(GROUPS),))
    mixed, routed = pl.pallas_call(
        kernel,
        out_shape=(pltpu.VMEM((TOK, D), jnp.bfloat16), pltpu.HBM((1,), jnp.int32)),
        in_specs=[hbm] * 6,
        out_specs=(vmem, smem),
        scratch_shapes=[
            pltpu.VMEM((TOK, D), jnp.bfloat16),
            pltpu.VMEM((1, TOK), jnp.int32),
            pltpu.VMEM((1, TOK), jnp.float32),
            pltpu.VMEM((1, D), jnp.float32),
            pltpu.VMEM((D, FF), jnp.bfloat16),
            pltpu.VMEM((FF, D), jnp.bfloat16),
            pltpu.VMEM((TOK, D), jnp.bfloat16),
            pltpu.VMEM((TOK, LANES), jnp.int32),
            slab,
            slab,
            slab,
            slab,
            pltpu.VMEM((MOST, FF), jnp.bfloat16),
            pltpu.VMEM((TOK, D), jnp.float32),
            pltpu.SemaphoreType.DMA((6,)),
            sems,
            sems,
            sems,
            sems,
        ],
        compiler_params=pltpu.CompilerParams(
            collective_id=0, has_side_effects=True, vmem_limit_bytes=VMEM_LIMIT
        ),
    )(
        *(
            pltpu.with_memory_space_constraint(a, pltpu.HBM)
            for a in (
                tokens,
                expert_ids.reshape(1, TOK),
                gate_prob.reshape(1, TOK),
                norm_gain.reshape(1, D),
                weight_in,
                weight_out,
            )
        )
    )
    return pl.pallas_call(
        put_out,
        out_shape=outs,
        in_specs=[vmem, hbm],
        out_specs=(hbm, hbm),
        scratch_shapes=[pltpu.SemaphoreType.DMA((2,))],
        compiler_params=pltpu.CompilerParams(vmem_limit_bytes=8 * 2**20),
    )(mixed, routed)


def solution(mesh):
    return jax.shard_map(
        on_device,
        mesh=mesh,
        in_specs=(
            P(ROW_COL, None),
            P(ROW_COL, None),
            P(ROW_COL),
            P(),
            P(ROW_COL, None, None),
            P(ROW_COL, None, None),
        ),
        out_specs=(P(ROW_COL, None), P(ROW_COL)),
        check_vma=False,
    )
```

time: 70.6 us -> 62.3 us (0.88)
  Pallas kernels: 65.8 us -> 61.6 us
  local copies, waits for them, and re-layouts: 2.26 us -> 0 us
  between operations: 2.33 us -> 0.64 us
    pallas_call x1 -> x2, Pallas kernels: 65.8 us -> 61.6 us  [the longest x1 60 us: on_device(): pl.pallas_call(kernel, out_shape=(pltpu.VMEM((TOK, D), jnp.bfloat16), plt...]
    unnamed x1 -> x0, local copies, waits for them, and re-layouts: 2.26 us -> none
where the time goes in v2:
time: 62.3 us; the launch traced here: 62.2 us
  Pallas kernels  61.6 us (99%)
  between operations  0.64 us (1%)
    pallas_call x1, Pallas kernels, on_device(): pl.pallas_call(kernel, out_shape=(pltpu.VMEM((TOK, D), jnp.bfloat16), plt...  60 us
    pallas_call x1, Pallas kernels, on_device(): pl.pallas_call(put_out, out_shape=outs, in_specs=[vmem, hbm], out_specs=(...  1.55 us

profile of v2, /device:TPU:1, one launch (start us, length us, event | category | flops | bytes accessed | tf_op | source)
XLA Modules:
  0.0 62.2 jit_solution(17535444855957455966)
XLA Ops:
  0.6 60.0 %shard_map.77 = (bf16[512,1024]{1,0:T(8,128)(2,1)S(1)}, s32[1]{0:T(128)}) custom-call(bf16[512,1024]{1,0:T(8,128)(2,1)} %tok_hbm.1, s32[1,512]{1,0:T(1,128)} %bitcast.4, f32[1,512]{1,0:T(1,128)} %bitcast.5, f32[1,1024]{1,0:T(1,128)} %bitcast.3, bf16[1,1024,4096]{2,1,0:T(8,128)(2,1)} %w1_hbm.1, bf16[1,4096,1024]{2,1,0:T(8,128)(2,1)} %w2_hbm.1), custom_call_target="tpu_custom_call" | custom-call | tf_op jit(solution)/shard_map/pallas_call | solution.py:255
  60.7 1.5 %shard_map.78 = (bf16[512,1024]{1,0:T(8,128)(2,1)}, s32[1]{0:T(128)}) custom-call(bf16[512,1024]{1,0:T(8,128)(2,1)S(1)} %get-tuple-element.4.mixed, s32[1]{0:T(128)} %get-tuple-element.5.count), custom_call_target="tpu_custom_call" | custom-call | tf_op jit(solution)/shard_map/pallas_call | solution.py:297

commit v3 on v2

--- a/solution.py
+++ b/solution.py
@@ -13,19 +13,21 @@
 CAP = 8
 PEERS = 128
 SLOTS = PEERS * CAP
-CLASSES = 4
-CLASS = PEERS // CLASSES
-GROUPS = ((0, 32), (32, 32), (64, 32), (96, 32))
+CLASS = PEERS // 4
+GROUPS = ((0, 16), (16, 32), (48, 32), (80, 32), (112, 16))
+PIECES = ((0, 16), (16, 16), (32, 32), (64, 32), (96, 32))
 MOST = max(count for _, count in GROUPS) * CAP
 EMPTY = 1024.0
 FF_TILE = 512
 D_TILE = 256
 LANES = 128
+OUT_PIECES = 4
 VMEM_LIMIT = 44 * 2**20
 
 
 def offset(k):
-    dx, dy, dc = k // 8 % 4, k // 2 % 4, k % 2
+    dx, dc = k // 4 % 4, k % 2
+    dy = (dx - k // 16 % 2 * 2 - k // 2 % 2) % 4
     return dx, dy, (k // CLASS - dx - dy) % 4, dc
 
 
@@ -134,7 +136,9 @@
     dc = ((ids_row >> 4) - here.core) & 1
     dy = ((ids_row >> 2) - here.y) & 3
     dz = (ids_row - here.z) & 3
-    slot_row = (((dx + dy + dz) & 3) * CLASS + dx * 8 + dy * 2 + dc) * CAP + within
+    turn = (dx - dy) & 3
+    inside = (turn >> 1) * 16 + dx * 4 + (turn & 1) * 2 + dc
+    slot_row = (((dx + dy + dz) & 3) * CLASS + inside) * CAP + within
     slot_cols[...] = columns(slot_row)
 
     loads[1].wait()
@@ -146,20 +150,20 @@
         normed[rows, :] = (wide * scale * gain[...]).astype(jnp.bfloat16)
 
     ones = jnp.ones((TOK, LANES), jnp.bfloat16)
-    rows = CLASS * CAP
-    for c in range(CLASSES):
-        places = lax.broadcasted_iota(jnp.int32, (rows, TOK), 0) + c * rows
+    for first, count in PIECES:
+        rows = count * CAP
+        places = lax.broadcasted_iota(jnp.int32, (rows, TOK), 0) + first * CAP
         table = jnp.where(slot_row == places, 1.0, 0.0).astype(jnp.bfloat16)
         filled = jnp.dot(table, ones, preferred_element_type=jnp.float32)
         values = jnp.dot(table, normed[...], preferred_element_type=jnp.float32)
         first_lane = lax.broadcasted_iota(jnp.int32, (rows, LANES), 1) == 0
         head = jnp.where(first_lane & (filled == 0.0), EMPTY, values[:, :LANES])
-        part = pl.ds(c * CLASS, CLASS)
-        outgoing[part, :, :LANES] = head.astype(jnp.bfloat16).reshape(CLASS, CAP, LANES)
-        outgoing[part, :, LANES:] = values[:, LANES:].astype(jnp.bfloat16).reshape(CLASS, CAP, D - LANES)
-        if c == 0:
+        part = pl.ds(first, count)
+        outgoing[part, :, :LANES] = head.astype(jnp.bfloat16).reshape(count, CAP, LANES)
+        outgoing[part, :, LANES:] = values[:, LANES:].astype(jnp.bfloat16).reshape(count, CAP, D - LANES)
+        if first == 0:
             pl.semaphore_wait(barrier, PEERS - 1)
-        for k in range(max(c * CLASS, 1), (c + 1) * CLASS):
+        for k in range(max(first, 1), first + count):
             pltpu.make_async_remote_copy(
                 src_ref=outgoing.at[k],
                 dst_ref=arrived.at[k],
@@ -224,25 +228,31 @@
         back = jnp.dot(pick, block, preferred_element_type=jnp.float32)
         if g == 0:
             total[...] = back
-        elif g < len(GROUPS) - 1:
+        elif g < len(GROUPS) - 2:
             total[...] += back
         else:
             for j in range(D // LANES):
                 cols = slice(j * LANES, (j + 1) * LANES)
-                got = gate_cols * (total[:, cols] + back[:, cols])
-                out_ref[:, cols] = (tok[:, cols].astype(jnp.float32) + got).astype(jnp.bfloat16)
+                if g < len(GROUPS) - 1:
+                    got = gate_cols * (total[:, cols] + back[:, cols])
+                    total[:, cols] = tok[:, cols].astype(jnp.float32) + got
+                else:
+                    out_ref[:, cols] = (total[:, cols] + gate_cols * back[:, cols]).astype(jnp.bfloat16)
     for g in range(len(GROUPS)):
         pltpu.make_async_copy(outgoing.at[moved(g)], arrived.at[moved(g)], send_out.at[g]).wait()
         pltpu.make_async_copy(answers.at[moved(g)], returned.at[moved(g)], send_back.at[g]).wait()
 
 
 def put_out(mixed, count, mixed_out, count_out, sem):
-    first = pltpu.make_async_copy(mixed, mixed_out, sem.at[0])
-    second = pltpu.make_async_copy(count, count_out, sem.at[1])
-    first.start()
-    second.start()
-    first.wait()
-    second.wait()
+    step = TOK // OUT_PIECES
+    copies = [pltpu.make_async_copy(count, count_out, sem.at[OUT_PIECES])]
+    for n in range(OUT_PIECES):
+        rows = pl.ds(n * step, step)
+        copies.append(pltpu.make_async_copy(mixed.at[rows], mixed_out.at[rows], sem.at[n]))
+    for copy in copies:
+        copy.start()
+    for copy in copies:
+        copy.wait()
 
 
 def on_device(tokens, expert_ids, gate_prob, norm_gain, weight_in, weight_out):
@@ -254,7 +264,7 @@
     sems = pltpu.SemaphoreType.DMA((len(GROUPS),))
     mixed, routed = pl.pallas_call(
         kernel,
-        out_shape=(pltpu.VMEM((TOK, D), jnp.bfloat16), pltpu.HBM((1,), jnp.int32)),
+        out_shape=(pltpu.VMEM((TOK, D), jnp.bfloat16), pltpu.SMEM((1,), jnp.int32)),
         in_specs=[hbm] * 6,
         out_specs=(vmem, smem),
         scratch_shapes=[
@@ -297,9 +307,9 @@
     return pl.pallas_call(
         put_out,
         out_shape=outs,
-        in_specs=[vmem, hbm],
+        in_specs=[vmem, smem],
         out_specs=(hbm, hbm),
-        scratch_shapes=[pltpu.SemaphoreType.DMA((2,))],
+        scratch_shapes=[pltpu.SemaphoreType.DMA((OUT_PIECES + 1,))],
         compiler_params=pltpu.CompilerParams(vmem_limit_bytes=8 * 2**20),
     )(mixed, routed)
 

time: 62.3 us -> 61.5 us (0.987)
  Pallas kernels: 61.6 us -> 60.7 us
where the time goes in v3:
time: 61.5 us; the launch traced here: 61.3 us
  Pallas kernels  60.7 us (99%)
  between operations  0.64 us (1%)
    pallas_call x1, Pallas kernels, on_device(): pl.pallas_call(kernel, out_shape=(pltpu.VMEM((TOK, D), jnp.bfloat16), plt...  59.7 us

profile of v3, /device:TPU:1, one launch (start us, length us, event | category | flops | bytes accessed | tf_op | source)
XLA Modules:
  0.0 61.3 jit_solution(2387767730476062433)
XLA Ops:
  0.6 59.7 %shard_map.77 = (bf16[512,1024]{1,0:T(8,128)(2,1)S(1)}, s32[1]{0:T(128)S(4)}) custom-call(bf16[512,1024]{1,0:T(8,128)(2,1)} %tok_hbm.1, s32[1,512]{1,0:T(1,128)} %bitcast.4, f32[1,512]{1,0:T(1,128)} %bitcast.5, f32[1,1024]{1,0:T(1,128)} %bitcast.3, bf16[1,1024,4096]{2,1,0:T(8,128)(2,1)} %w1_hbm.1, bf16[1,4096,1024]{2,1,0:T(8,128)(2,1)} %w2_hbm.1), custom_call_target="tpu_custom_call" | custom-call | tf_op jit(solution)/shard_map/pallas_call | solution.py:265
  60.3 1.0 %shard_map.78 = (bf16[512,1024]{1,0:T(8,128)(2,1)}, s32[1]{0:T(128)}) custom-call(bf16[512,1024]{1,0:T(8,128)(2,1)S(1)} %get-tuple-element.4.mixed, s32[1]{0:T(128)S(4)} %get-tuple-element.5.count), custom_call_target="tpu_custom_call" | custom-call | tf_op jit(solution)/shard_map/pallas_call | solution.py:307

commit v4 on v3

--- a/solution.py
+++ b/solution.py
@@ -17,6 +17,7 @@
 GROUPS = ((0, 16), (16, 32), (48, 32), (80, 32), (112, 16))
 PIECES = ((0, 16), (16, 16), (32, 32), (64, 32), (96, 32))
 MOST = max(count for _, count in GROUPS) * CAP
+LAST = GROUPS[-1][1] * CAP
 EMPTY = 1024.0
 FF_TILE = 512
 D_TILE = 256
@@ -77,7 +78,10 @@
     gain_hbm,
     w1_hbm,
     w2_hbm,
-    out_ref,
+    total,
+    last,
+    last_pick,
+    gate_cols_ref,
     routed_ref,
     tok,
     ids,
@@ -92,7 +96,6 @@
     answers,
     returned,
     hidden,
-    total,
     load_sem,
     send_out,
     recv_out,
@@ -225,6 +228,11 @@
         pick = jnp.concatenate(picks, axis=1)
         pltpu.make_async_copy(answers.at[moved(g)], returned.at[moved(g)], recv_back.at[g]).wait()
         block = returned[pl.ds(first, count)].reshape(count * CAP, D)
+        if g == len(GROUPS) - 1:
+            last[...] = block
+            last_pick[...] = pick
+            gate_cols_ref[...] = gate_cols
+            continue
         back = jnp.dot(pick, block, preferred_element_type=jnp.float32)
         if g == 0:
             total[...] = back
@@ -233,24 +241,25 @@
         else:
             for j in range(D // LANES):
                 cols = slice(j * LANES, (j + 1) * LANES)
-                if g < len(GROUPS) - 1:
-                    got = gate_cols * (total[:, cols] + back[:, cols])
-                    total[:, cols] = tok[:, cols].astype(jnp.float32) + got
-                else:
-                    out_ref[:, cols] = (total[:, cols] + gate_cols * back[:, cols]).astype(jnp.bfloat16)
+                got = gate_cols * (total[:, cols] + back[:, cols])
+                total[:, cols] = tok[:, cols].astype(jnp.float32) + got
     for g in range(len(GROUPS)):
         pltpu.make_async_copy(outgoing.at[moved(g)], arrived.at[moved(g)], send_out.at[g]).wait()
         pltpu.make_async_copy(answers.at[moved(g)], returned.at[moved(g)], send_back.at[g]).wait()
 
 
-def put_out(mixed, count, mixed_out, count_out, sem):
+def finish(total, last, pick, gate_cols, count, mixed_out, count_out, mixed, sem):
     step = TOK // OUT_PIECES
     copies = [pltpu.make_async_copy(count, count_out, sem.at[OUT_PIECES])]
+    copies[0].start()
     for n in range(OUT_PIECES):
         rows = pl.ds(n * step, step)
+        back = jnp.dot(pick[rows, :], last[...], preferred_element_type=jnp.float32)
+        for j in range(D // LANES):
+            cols = slice(j * LANES, (j + 1) * LANES)
+            mixed[rows, cols] = (total[rows, cols] + gate_cols[rows, :] * back[:, cols]).astype(jnp.bfloat16)
         copies.append(pltpu.make_async_copy(mixed.at[rows], mixed_out.at[rows], sem.at[n]))
-    for copy in copies:
-        copy.start()
+        copies[-1].start()
     for copy in copies:
         copy.wait()
 
@@ -262,11 +271,17 @@
     outs = (jax.ShapeDtypeStruct((TOK, D), jnp.bfloat16), jax.ShapeDtypeStruct((1,), jnp.int32))
     slab = pltpu.VMEM((PEERS, CAP, D), jnp.bfloat16)
     sems = pltpu.SemaphoreType.DMA((len(GROUPS),))
-    mixed, routed = pl.pallas_call(
+    *parts, routed = pl.pallas_call(
         kernel,
-        out_shape=(pltpu.VMEM((TOK, D), jnp.bfloat16), pltpu.SMEM((1,), jnp.int32)),
+        out_shape=(
+            pltpu.VMEM((TOK, D), jnp.float32),
+            pltpu.VMEM((LAST, D), jnp.bfloat16),
+            pltpu.VMEM((TOK, LAST), jnp.bfloat16),
+            pltpu.VMEM((TOK, LANES), jnp.float32),
+            pltpu.SMEM((1,), jnp.int32),
+        ),
         in_specs=[hbm] * 6,
-        out_specs=(vmem, smem),
+        out_specs=(vmem, vmem, vmem, vmem, smem),
         scratch_shapes=[
             pltpu.VMEM((TOK, D), jnp.bfloat16),
             pltpu.VMEM((1, TOK), jnp.int32),
@@ -281,7 +296,6 @@
             slab,
             slab,
             pltpu.VMEM((MOST, FF), jnp.bfloat16),
-            pltpu.VMEM((TOK, D), jnp.float32),
             pltpu.SemaphoreType.DMA((6,)),
             sems,
             sems,
@@ -305,13 +319,13 @@
         )
     )
     return pl.pallas_call(
-        put_out,
+        finish,
         out_shape=outs,
-        in_specs=[vmem, smem],
+        in_specs=[vmem, vmem, vmem, vmem, smem],
         out_specs=(hbm, hbm),
-        scratch_shapes=[pltpu.SemaphoreType.DMA((OUT_PIECES + 1,))],
+        scratch_shapes=[pltpu.VMEM((TOK, D), jnp.bfloat16), pltpu.SemaphoreType.DMA((OUT_PIECES + 1,))],
         compiler_params=pltpu.CompilerParams(vmem_limit_bytes=8 * 2**20),
-    )(mixed, routed)
+    )(*parts, routed)
 
 
 def solution(mesh):

time: 61.5 us -> 61.3 us (level)
  no operation moved by 1% of the time
where the time goes in v4:
time: 61.3 us; the launch traced here: 61.2 us
  Pallas kernels  60.6 us (99%)
  between operations  0.64 us (1%)
    pallas_call x1, Pallas kernels, on_device(): pl.pallas_call(kernel, out_shape=(pltpu.VMEM((TOK, D), jnp.float32), pltp...  59.3 us
    pallas_call x1, Pallas kernels, on_device(): pl.pallas_call(finish, out_shape=outs, in_specs=[vmem, vmem, vmem, vmem,...  1.23 us

profile of v4, /device:TPU:1, one launch (start us, length us, event | category | flops | bytes accessed | tf_op | source)
XLA Modules:
  0.0 61.2 jit_solution(16617381316486425008)
XLA Ops:
  0.6 59.3 %shard_map.77 = (f32[512,1024]{1,0:T(8,128)S(1)}, bf16[128,1024]{1,0:T(8,128)(2,1)S(1)}, bf16[512,128]{1,0:T(8,128)(2,1)S(1)}, f32[512,128]{1,0:T(8,128)S(1)}, s32[1]{0:T(128)S(4)}) custom-call(bf16[512,1024]{1,0:T(8,128)(2,1)} %tok_hbm.1, s32[1,512]{1,0:T(1,128)} %bitcast.4, f32[1,512]{1,0:T(1,128)} %bitcast.5, f32[1,1024]{1,0:T(1,128)} %bitcast.3, ...), custom_call_target="tpu_custom_call" | custom-call | tf_op jit(solution)/shard_map/pallas_call | solution.py:274
  60.0 1.2 %shard_map.78 = (bf16[512,1024]{1,0:T(8,128)(2,1)}, s32[1]{0:T(128)}) custom-call(f32[512,1024]{1,0:T(8,128)S(1)} %get-tuple-element.7.total, bf16[128,1024]{1,0:T(8,128)(2,1)S(1)} %get-tuple-element.8.last, bf16[512,128]{1,0:T(8,128)(2,1)S(1)} %get-tuple-element.9.pick, f32[512,128]{1,0:T(8,128)S(1)} %get-tuple-element.10.gate_cols, ...), custom_call_target="tpu_custom_call" | custom-call | tf_op jit(solution)/shard_map/pallas_call | solution.py:321

commit v5 on v4

--- a/solution.py
+++ b/solution.py
@@ -226,12 +226,13 @@
             lane = lax.broadcasted_iota(jnp.int32, (TOK, LANES), 1) + (first * CAP + j * LANES)
             picks.append(jnp.where(slot_cols[...] == lane, 1.0, 0.0).astype(jnp.bfloat16))
         pick = jnp.concatenate(picks, axis=1)
+        if g == len(GROUPS) - 1:
+            last_pick[...] = pick
+            gate_cols_ref[...] = gate_cols
         pltpu.make_async_copy(answers.at[moved(g)], returned.at[moved(g)], recv_back.at[g]).wait()
         block = returned[pl.ds(first, count)].reshape(count * CAP, D)
         if g == len(GROUPS) - 1:
             last[...] = block
-            last_pick[...] = pick
-            gate_cols_ref[...] = gate_cols
             continue
         back = jnp.dot(pick, block, preferred_element_type=jnp.float32)
         if g == 0:

time: 61.3 us -> 61.3 us (level)
  no operation moved by 1% of the time
where the time goes in v5:
time: 61.3 us; the launch traced here: 61.2 us
  Pallas kernels  60.6 us (99%)
  between operations  0.64 us (1%)
    pallas_call x1, Pallas kernels, on_device(): pl.pallas_call(kernel, out_shape=(pltpu.VMEM((TOK, D), jnp.float32), pltp...  59.3 us
    pallas_call x1, Pallas kernels, on_device(): pl.pallas_call(finish, out_shape=outs, in_specs=[vmem, vmem, vmem, vmem,...  1.23 us

profile of v5, /device:TPU:1, one launch (start us, length us, event | category | flops | bytes accessed | tf_op | source)
XLA Modules:
  0.0 61.2 jit_solution(8517797049711062385)
XLA Ops:
  0.6 59.3 %shard_map.77 = (f32[512,1024]{1,0:T(8,128)S(1)}, bf16[128,1024]{1,0:T(8,128)(2,1)S(1)}, bf16[512,128]{1,0:T(8,128)(2,1)S(1)}, f32[512,128]{1,0:T(8,128)S(1)}, s32[1]{0:T(128)S(4)}) custom-call(bf16[512,1024]{1,0:T(8,128)(2,1)} %tok_hbm.1, s32[1,512]{1,0:T(1,128)} %bitcast.4, f32[1,512]{1,0:T(1,128)} %bitcast.5, f32[1,1024]{1,0:T(1,128)} %bitcast.3, ...), custom_call_target="tpu_custom_call" | custom-call | tf_op jit(solution)/shard_map/pallas_call | solution.py:275
  60.0 1.2 %shard_map.78 = (bf16[512,1024]{1,0:T(8,128)(2,1)}, s32[1]{0:T(128)}) custom-call(f32[512,1024]{1,0:T(8,128)S(1)} %get-tuple-element.7.total, bf16[128,1024]{1,0:T(8,128)(2,1)S(1)} %get-tuple-element.8.last, bf16[512,128]{1,0:T(8,128)(2,1)S(1)} %get-tuple-element.9.pick, f32[512,128]{1,0:T(8,128)S(1)} %get-tuple-element.10.gate_cols, ...), custom_call_target="tpu_custom_call" | custom-call | tf_op jit(solution)/shard_map/pallas_call | solution.py:322
